TPU v7x, 32 devices: a whole 2x2x4 slice. The times are simulated.
32 devices in a mesh: pat: 2 (over y), slab: 4 (over z), phase: 2 (over x), enc: 2 (over core).
Axes of the slice: x: 2, y: 2, z: 4, core: 2. Of those that a mesh axis runs over, the one named last changes fastest.
Arguments:
- kspace_data: bfloat16 [4, 2, 4, 96, 64, 192], P('pat', 'phase', 'enc', 'slab'), parts along dimension 0, may hold values from -6 to 6
- coil_maps: bfloat16 [4, 24, 4, 64, 192], P('pat', None, None, 'slab'), parts along dimension 0, may hold values from -1 to 1
- sampling: int32 [2, 4, 128, 192], P('phase', 'enc', 'pat'), parts along dimension 2, may hold values 0 or 1
Outputs:
- image_estimate: float32 [4, 2, 4, 4, 64, 192], P('pat', 'phase', 'enc', None, 'slab'), parts along dimension 0
- residual: float32 [4, 2, 4, 96, 64, 192], P('pat', 'phase', 'enc', 'slab'), parts along dimension 0
There are 2 independent parts, one for each index of `pat`. A program takes and returns all parts, laid end to end along the dimension named above; each array names one. Nothing has to cross between parts.
All inputs are finite; a program needn't handle non-finite values. No bound on the sum of `sampling` on one device may be relied on, other than what follows from the above.
Results may differ from a plain program's by a relative error of at most 0.0046.
Values may be sent and summed in bfloat16 or wider, within the bound.
A program may use at most 64 MiB of HBM per device.

v0:
```python
import math
import jax
import jax.numpy as jnp
from jax import lax
from jax.sharding import PartitionSpec as P

ITERS = 2
tv_weight = 0.15
smoothing = 0.6


def with_halo(value, sides, width):
    for axis, dim in sides:
        size, length = (lax.axis_size(axis), value.shape[dim])
        up = [(i, (i + 1) % size) for i in range(size)]
        down = [(j, i) for i, j in up]
        last = lax.slice_in_dim(value, length - width, length, axis=dim)
        first = lax.slice_in_dim(value, 0, width, axis=dim)
        before = lax.ppermute(last, axis, up)
        after = lax.ppermute(first, axis, down)
        value = jnp.concatenate([before, value, after], axis=dim)
    return value


def dft_table(length, direction):
    counter = jnp.arange(length, dtype=jnp.int32)
    product = counter[:, None] * counter[None, :] % length
    angle = product.astype(jnp.float32) * (2.0 * math.pi / length)
    factor = 1.0 / math.sqrt(length)
    return (
        (jnp.cos(angle) * factor).astype(jnp.bfloat16),
        (direction * jnp.sin(angle) * factor).astype(jnp.bfloat16),
    )


def along_rows(real_part, imag_part, table):
    cosine, sine = table
    real_out = jnp.matmul(real_part, cosine, preferred_element_type=jnp.float32) - jnp.matmul(
        imag_part, sine, preferred_element_type=jnp.float32
    )
    imag_out = jnp.matmul(real_part, sine, preferred_element_type=jnp.float32) + jnp.matmul(
        imag_part, cosine, preferred_element_type=jnp.float32
    )
    return (real_out, imag_out)


def along_depth(real_part, imag_part, table):
    cosine, sine = table
    real_out = jnp.einsum(
        "...zy,zw->...wy", real_part, cosine, preferred_element_type=jnp.float32
    ) - jnp.einsum("...zy,zw->...wy", imag_part, sine, preferred_element_type=jnp.float32)
    imag_out = jnp.einsum(
        "...zy,zw->...wy", real_part, sine, preferred_element_type=jnp.float32
    ) + jnp.einsum("...zy,zw->...wy", imag_part, cosine, preferred_element_type=jnp.float32)
    return (real_out, imag_out)


def coil_product(coil_real, coil_imag, real_in, imag_in, column_fwd):
    prod_real = (coil_real * real_in - coil_imag * imag_in).astype(jnp.bfloat16)
    prod_imag = (coil_real * imag_in + coil_imag * real_in).astype(jnp.bfloat16)
    mid_real, mid_imag = along_rows(prod_real, prod_imag, column_fwd)
    return jnp.stack([mid_real, mid_imag]).astype(jnp.bfloat16)


def body(kspace_data, coil_maps, sampling):
    phases = kspace_data.shape[1]
    encodings = kspace_data.shape[2]
    coils = coil_maps.shape[1]
    readout = coil_maps.shape[2]
    zdepth = coil_maps.shape[3]
    lines = coil_maps.shape[4]
    slices = kspace_data.shape[4]
    column_fwd = dft_table(lines, -1.0)
    depth_fwd = dft_table(slices, -1.0)
    column_inv = dft_table(lines, 1.0)
    depth_inv = dft_table(slices, 1.0)
    coil_real = coil_maps[0].astype(jnp.float32)
    coil_imag = coil_maps[1].astype(jnp.float32)
    sampled = sampling.astype(jnp.float32)[None, :, :, None]
    residual = -(kspace_data.astype(jnp.float32) * sampled)
    image_estimate = jnp.zeros((2, phases, encodings, readout, zdepth, lines), jnp.float32)
    row_count = kspace_data.shape[3]
    coil_rows = lax.all_to_all(
        coil_maps.reshape(2, coils * readout, zdepth, lines),
        "slab",
        split_axis=1,
        concat_axis=2,
        tiled=True,
    )
    row_columns = (
        lax.axis_index("slab") * row_count + jnp.arange(row_count, dtype=jnp.int32)
    ) % readout
    for iteration in range(ITERS):
        low = residual.astype(jnp.bfloat16)
        inv_real, inv_imag = along_depth(low[0], low[1], depth_inv)
        partial_rows = jnp.stack([inv_real, inv_imag]).astype(jnp.bfloat16)
        portion = lax.all_to_all(partial_rows, "slab", split_axis=4, concat_axis=3, tiled=True)
        shaped = portion.reshape(
            2,
            portion.shape[1],
            portion.shape[2],
            coils,
            readout,
            portion.shape[4],
            portion.shape[5],
        )
        fine_real, fine_imag = along_rows(shaped[0], shaped[1], column_inv)
        grad_real = jnp.sum(coil_real * fine_real + coil_imag * fine_imag, axis=2)
        grad_imag = jnp.sum(coil_real * fine_imag - coil_imag * fine_real, axis=2)
        adjoint = jnp.stack([grad_real, grad_imag])
        padded = with_halo(image_estimate, (("phase", 1),), 1)
        difference = padded[:, 1:] - padded[:, :-1]
        modulus = difference[0] * difference[0] + difference[1] * difference[1]
        weights = difference / jnp.sqrt(modulus + smoothing * smoothing)[None]
        gradient = adjoint + tv_weight * (weights[:, :-1] - weights[:, 1:])
        grad_local = jnp.sum(gradient * gradient)
        grad_sq = lax.psum(grad_local, ("slab", "phase", "enc"))
        low_grad = gradient.astype(jnp.bfloat16)
        picked = jnp.take(
            lax.all_gather(low_grad, "slab", axis=4, tiled=True), row_columns, axis=3
        ).astype(jnp.float32)
        local_coils = coil_rows.astype(jnp.float32)
        mid = coil_product(local_coils[0], local_coils[1], picked[0], picked[1], column_fwd)
        out_real, out_imag = along_depth(mid[0], mid[1], depth_fwd)
        spectrum = jnp.stack([out_real, out_imag])
        spectrum = spectrum * sampled
        spec_local = jnp.sum(spectrum * spectrum)
        spec_sq = lax.psum(spec_local, ("slab", "phase", "enc"))
        alpha = grad_sq / (spec_sq + 4.0 * tv_weight / smoothing * grad_sq + 1e-06)
        image_estimate = image_estimate - alpha * gradient
        residual = residual - alpha * spectrum
    return (image_estimate, residual)


def solution(mesh):
    in_specs = (
        P("pat", "phase", "enc", "slab", None, None),
        P("pat", None, None, "slab", None),
        P("phase", "enc", "pat", None),
    )
    out_specs = (
        P("pat", "phase", "enc", None, "slab", None),
        P("pat", "phase", "enc", "slab", None, None),
    )
    return jax.shard_map(body, mesh=mesh, in_specs=in_specs, out_specs=out_specs, check_vma=False)
```

profile of v0, /device:TPU:0, one launch (start us, length us, event | category | flops | bytes accessed | tf_op | source)
XLA Modules:
  0.0 373.4 jit_solution(6726968447215893808)
XLA Ops:
  0.7 2.9 copy.52
  3.6 6.3 %all-to-all-start.1 = ((bf16[2,96,16,192]{3,2,0,1:T(8,128)(2,1)}), bf16[2,96,16,192]{3,2,0,1:T(8,128)(2,1)}, u32[]{:S(2)}, u32[]{:S(2)}) async-start(bf16[2,96,16,192]{3,2,0,1:T(8,128)(2,1)} %bitcast.243), calls=%async_computation.1 | async-start | bytes 3145728 | tf_op jit(solution)/shard_map/all_to_all | solution.py:83
  14.2 3.4 copy.50
  17.7 29.3 %all-to-all-done.1 = bf16[2,96,16,192]{3,2,0,1:T(8,128)(2,1)} async-done(((bf16[2,96,16,192]{3,2,0,1:T(8,128)(2,1)}), bf16[2,96,16,192]{3,2,0,1:T(8,128)(2,1)}, u32[]{:S(2)}, u32[]{:S(2)}) %all-to-all-start.1) | async-done | bytes 1179680 | tf_op jit(solution)/shard_map/all_to_all | solution.py:83
  47.0 4.8 %all-to-all-start = ((bf16[2,1,2,24,64,192]{5,3,2,1,0,4:T(8,128)(2,1)}), bf16[2,1,2,24,64,192]{5,3,2,1,0,4:T(8,128)(2,1)}, u32[]{:S(2)}, u32[]{:S(2)}) async-start(bf16[2,1,2,24,64,192]{5,3,2,1,0,4:T(8,128)(2,1)} %copy.50), calls=%async_computation | async-start | bytes 6291456 | tf_op jit(solution)/shard_map/all_to_all | solution.py:97
  56.4 5.5 %collective-permute-done = f32[2,1,2,4,16,192]{5,4,3,2,0,1:T(8,128)S(1)} collective-permute-done((f32[2,1,2,4,16,192]{5,4,3,2,0,1:T(8,128)}, f32[2,1,2,4,16,192]{5,4,3,2,0,1:T(8,128)S(1)}, u32[]{:S(2)}, u32[]{:S(2)}) %collective-permute-start) | collective-permute-done | bytes 196640 | tf_op jit(solution)/shard_map/ppermute | solution.py:20
  61.9 3.9 %collective-permute-done.1 = f32[2,1,2,4,16,192]{5,4,3,2,0,1:T(8,128)} collective-permute-done((f32[2,1,2,4,16,192]{5,4,3,2,0,1:T(8,128)}, f32[2,1,2,4,16,192]{5,4,3,2,0,1:T(8,128)}, u32[]{:S(2)}, u32[]{:S(2)}) %collective-permute-start.1) | collective-permute-done | bytes 196640 | tf_op jit(solution)/shard_map/ppermute | solution.py:19
  73.7 48.4 %all-to-all-done = bf16[2,1,2,24,64,192]{5,3,2,1,0,4:T(8,128)(2,1)} async-done(((bf16[2,1,2,24,64,192]{5,3,2,1,0,4:T(8,128)(2,1)}), bf16[2,1,2,24,64,192]{5,3,2,1,0,4:T(8,128)(2,1)}, u32[]{:S(2)}, u32[]{:S(2)}) %all-to-all-start) | async-done | bytes 2359328 | tf_op jit(solution)/shard_map/all_to_all | solution.py:97
  122.1 3.7 copy.96
  132.4 16.1 %all_gather.6 = bf16[2,1,2,4,64,192]{5,4,3,2,0,1:T(8,128)(2,1)S(1)} all-gather(bf16[2,1,2,4,16,192]{5,4,3,2,0,1:T(8,128)(2,1)S(1)} %get-tuple-element.19), channel_id=1, replica_groups=mesh['pat'=2,'slab'=4,'phase'=2,'enc'=2] {'slab'}, dimensions={4}, use_global_device_ids=true | all-gather | bytes 491520 | tf_op jit(solution)/shard_map/all_gather | solution.py:120
  148.5 2.5 gather_fusion
  166.1 30.6 %all-reduce.3 = (f32[]{:T(128)}, f32[]{:T(128)}) all-reduce(f32[]{:T(128)} %multiply_reduce_fusion.3, f32[]{:T(128)} %multiply_reduce_fusion.1), channel_id=1, replica_groups=mesh['pat'=2,'slab'=4,'phase'=2,'enc'=2] {'slab','phase','enc'}, use_global_device_ids=true, to_apply=%region_3.4 | all-reduce | flops 2 | bytes 16 | tf_op jit(solution)/shard_map/psum | solution.py:117
  198.6 3.6 fusion.3
  205.6 3.4 copy.60
  209.1 4.6 %all-to-all-start.2 = ((bf16[2,1,2,24,64,192]{5,3,2,1,0,4:T(8,128)(2,1)}), bf16[2,1,2,24,64,192]{5,3,2,1,0,4:T(8,128)(2,1)}, u32[]{:S(2)}, u32[]{:S(2)}) async-start(bf16[2,1,2,24,64,192]{5,3,2,1,0,4:T(8,128)(2,1)} %copy.60), calls=%async_computation.2 | async-start | bytes 6291456 | tf_op jit(solution)/shard_map/all_to_all | solution.py:97
  215.8 7.2 %collective-permute-done.2 = f32[2,1,2,4,16,192]{5,4,3,2,0,1:T(8,128)S(1)} collective-permute-done((f32[2,1,2,4,16,192]{5,4,3,2,0,1:T(8,128)S(1)}, f32[2,1,2,4,16,192]{5,4,3,2,0,1:T(8,128)S(1)}, u32[]{:S(2)}, u32[]{:S(2)}) %collective-permute-start.2) | collective-permute-done | bytes 196640 | tf_op jit(solution)/shard_map/ppermute | solution.py:20
  223.0 4.5 %collective-permute-done.3 = f32[2,1,2,4,16,192]{5,4,3,2,0,1:T(8,128)S(1)} collective-permute-done((f32[2,1,2,4,16,192]{5,4,3,2,0,1:T(8,128)S(1)}, f32[2,1,2,4,16,192]{5,4,3,2,0,1:T(8,128)S(1)}, u32[]{:S(2)}, u32[]{:S(2)}) %collective-permute-start.3) | collective-permute-done | bytes 196640 | tf_op jit(solution)/shard_map/ppermute | solution.py:19
  228.6 56.1 %all-to-all-done.2 = bf16[2,1,2,24,64,192]{5,3,2,1,0,4:T(8,128)(2,1)} async-done(((bf16[2,1,2,24,64,192]{5,3,2,1,0,4:T(8,128)(2,1)}), bf16[2,1,2,24,64,192]{5,3,2,1,0,4:T(8,128)(2,1)}, u32[]{:S(2)}, u32[]{:S(2)}) %all-to-all-start.2) | async-done | bytes 2359328 | tf_op jit(solution)/shard_map/all_to_all | solution.py:97
  284.7 3.7 copy.95
  296.4 17.0 %all_gather.7 = bf16[2,1,2,4,64,192]{5,4,3,2,0,1:T(8,128)(2,1)} all-gather(bf16[2,1,2,4,16,192]{5,4,3,2,0,1:T(8,128)(2,1)S(1)} %get-tuple-element.17), channel_id=1, replica_groups=mesh['pat'=2,'slab'=4,'phase'=2,'enc'=2] {'slab'}, dimensions={4}, use_global_device_ids=true | all-gather | bytes 491520 | tf_op jit(solution)/shard_map/all_gather | solution.py:120
  313.4 3.6 gather_fusion.1
  317.0 2.6 fusion.1
  332.9 30.1 %all-reduce.2 = (f32[]{:T(128)}, f32[]{:T(128)}) all-reduce(f32[]{:T(128)} %multiply_reduce_fusion.2, f32[]{:T(128)} %multiply_reduce_fusion), channel_id=1, replica_groups=mesh['pat'=2,'slab'=4,'phase'=2,'enc'=2] {'slab','phase','enc'}, use_global_device_ids=true, to_apply=%region_9.11 | all-reduce | flops 2 | bytes 16 | tf_op jit(solution)/shard_map/psum | solution.py:117
  365.0 7.4 %multiply_subtract_fusion = f32[2,1,2,24,64,192]{5,4,3,2,1,0:T(8,128)} fusion(f32[1,1,2,24,64,192]{5,4,3,2,1,0:T(8,128)} %copy-done.7, f32[1,1,2,24,64,192]{5,4,3,2,1,0:T(8,128)} %copy-done.6, f32[]{:T(128)S(6)} %div.33, f32[2,64,192]{2,1,0:T(8,128)S(1)} %convert_bitcast_fusion.1, f32[1,1,2,24,64,192]{5,4,3,2,1,0:T(8,128)} %copy-done, ...), kind=kLoop, calls=%fused_computation.4 | loop fusion | flops 12976128 | bytes 16613384 | tf_op jit(solution)/shard_map/sub | solution.py:131
  (101 shorter events, 67.0 us)
Async XLA Ops:
  0.6 9.3 %copy-start.16 = (s32[1,2,64,192]{3,2,1,0:T(8,128)S(1)}, s32[1,2,64,192]{3,2,1,0:T(8,128)}, u32[]{:S(2)}) copy-start(s32[1,2,64,192]{3,2,1,0:T(8,128)} %param.7) | copy-start | bytes 294916
  0.6 9.3 %copy-start.5 = (bf16[2,1,2,24,64,192]{5,4,3,2,1,0:T(8,128)(2,1)S(1)}, bf16[2,1,2,24,64,192]{5,4,3,2,1,0:T(8,128)(2,1)}, u32[]{:S(2)}) copy-start(bf16[2,1,2,24,64,192]{5,4,3,2,1,0:T(8,128)(2,1)} %param.5) | copy-start | bytes 7077892
  3.6 43.4 %all-to-all-start.1 = ((bf16[2,96,16,192]{3,2,0,1:T(8,128)(2,1)}), bf16[2,96,16,192]{3,2,0,1:T(8,128)(2,1)}, u32[]{:S(2)}, u32[]{:S(2)}) async-start(bf16[2,96,16,192]{3,2,0,1:T(8,128)(2,1)} %bitcast.243), calls=%async_computation.1 | async-start | bytes 3145728 | tf_op jit(solution)/shard_map/all_to_all | solution.py:83
  47.0 75.1 %all-to-all-start = ((bf16[2,1,2,24,64,192]{5,3,2,1,0,4:T(8,128)(2,1)}), bf16[2,1,2,24,64,192]{5,3,2,1,0,4:T(8,128)(2,1)}, u32[]{:S(2)}, u32[]{:S(2)}) async-start(bf16[2,1,2,24,64,192]{5,3,2,1,0,4:T(8,128)(2,1)} %copy.50), calls=%async_computation | async-start | bytes 6291456 | tf_op jit(solution)/shard_map/all_to_all | solution.py:97
  52.5 9.4 %collective-permute-start = (f32[2,1,2,4,16,192]{5,4,3,2,0,1:T(8,128)}, f32[2,1,2,4,16,192]{5,4,3,2,0,1:T(8,128)S(1)}, u32[]{:S(2)}, u32[]{:S(2)}) collective-permute-start(f32[2,1,2,4,16,192]{5,4,3,2,0,1:T(8,128)} %broadcast_in_dim.8), channel_id=1, source_target_pairs={{2,0},{0,2},{3,1},{1,3},{6,4},{4,6},{7,5},{5,7},{10,8},{8,10},{11,... | collective-permute-start | bytes 589832 | tf_op jit(solution)/shard_map/ppermute | solution.py:20
  54.0 11.8 %collective-permute-start.1 = (f32[2,1,2,4,16,192]{5,4,3,2,0,1:T(8,128)}, f32[2,1,2,4,16,192]{5,4,3,2,0,1:T(8,128)}, u32[]{:S(2)}, u32[]{:S(2)}) collective-permute-start(f32[2,1,2,4,16,192]{5,4,3,2,0,1:T(8,128)} %broadcast_in_dim.8), channel_id=1, source_target_pairs={{0,2},{2,0},{1,3},{3,1},{4,6},{6,4},{5,7},{7,5},{8,10},{10,8},{9,1... | collective-permute-start | bytes 589832 | tf_op jit(solution)/shard_map/ppermute | solution.py:19
  56.4 73.5 %copy-start.1 = (f32[24,4,16,192]{3,2,1,0:T(8,128)}, f32[24,4,16,192]{3,2,1,0:T(8,128)S(1)}, u32[]{:S(2)}) copy-start(f32[24,4,16,192]{3,2,1,0:T(8,128)S(1)} %get-tuple-element.31) | copy-start | bytes 3538948
  56.4 73.5 %copy-start.3 = (f32[24,4,16,192]{3,2,1,0:T(8,128)}, f32[24,4,16,192]{3,2,1,0:T(8,128)S(1)}, u32[]{:S(2)}) copy-start(f32[24,4,16,192]{3,2,1,0:T(8,128)S(1)} %get-tuple-element.32) | copy-start | bytes 3538948
  129.9 2.4 copy-start.15
  151.1 2.5 copy-start.8
  151.1 2.8 copy-start.10
  163.2 2.2 copy-start
  209.1 75.7 %all-to-all-start.2 = ((bf16[2,1,2,24,64,192]{5,3,2,1,0,4:T(8,128)(2,1)}), bf16[2,1,2,24,64,192]{5,3,2,1,0,4:T(8,128)(2,1)}, u32[]{:S(2)}, u32[]{:S(2)}) async-start(bf16[2,1,2,24,64,192]{5,3,2,1,0,4:T(8,128)(2,1)} %copy.60), calls=%async_computation.2 | async-start | bytes 6291456 | tf_op jit(solution)/shard_map/all_to_all | solution.py:97
  213.7 9.2 %collective-permute-start.2 = (f32[2,1,2,4,16,192]{5,4,3,2,0,1:T(8,128)S(1)}, f32[2,1,2,4,16,192]{5,4,3,2,0,1:T(8,128)S(1)}, u32[]{:S(2)}, u32[]{:S(2)}) collective-permute-start(f32[2,1,2,4,16,192]{5,4,3,2,0,1:T(8,128)S(1)} %multiply_subtract_fusion.2), channel_id=1, source_target_pairs={{2,0},{0,2},{3,1},{1,3},{6,4},{4,6},{7,5},{5,7},{10,8},{8,10},{11,... | collective-permute-start | bytes 589832 | tf_op jit(solution)/shard_map/ppermute | solution.py:20
  213.8 13.7 %collective-permute-start.3 = (f32[2,1,2,4,16,192]{5,4,3,2,0,1:T(8,128)S(1)}, f32[2,1,2,4,16,192]{5,4,3,2,0,1:T(8,128)S(1)}, u32[]{:S(2)}, u32[]{:S(2)}) collective-permute-start(f32[2,1,2,4,16,192]{5,4,3,2,0,1:T(8,128)S(1)} %multiply_subtract_fusion.2), channel_id=1, source_target_pairs={{0,2},{2,0},{1,3},{3,1},{4,6},{6,4},{5,7},{7,5},{8,10},{10,8},{9,1... | collective-permute-start | bytes 589832 | tf_op jit(solution)/shard_map/ppermute | solution.py:19
  291.3 1.4 copy-start.2
  291.3 1.9 copy-start.4
  293.2 2.4 copy-start.14
  317.0 2.6 copy-start.9
  317.0 2.8 copy-start.11
  328.3 1.7 copy-start.6
  330.0 2.3 copy-start.7
  330.0 2.3 copy-start.12
  365.0 7.4 %copy-start.13 = (f32[2,1,2,4,16,192]{5,4,3,2,0,1:T(8,128)S(1)}, f32[2,1,2,4,16,192]{5,4,3,2,0,1:T(8,128)}, u32[]{:S(2)}) copy-start(f32[2,1,2,4,16,192]{5,4,3,2,0,1:T(8,128)} %get-tuple-element.18) | copy-start | bytes 589828
where the time goes:
time: 379 us; the launch traced here: 373 us
  waiting for transfers between devices  155 us (41%)
  blocking collectives  93.8 us (25%)
  other arithmetic  35.8 us (9%)
  matrix products  34.2 us (9%)
  local copies, waits for them, and re-layouts  29.6 us (8%)
  starting transfers between devices  19.9 us (5%)
  between operations  5.16 us (1%)
    all_to_all x2, waiting for transfers between devices, body(): lax.all_to_all(partial_rows, 'slab', split_axis=4, concat_axis=3, tiled=T...  105 us
    psum x2, blocking collectives, body(): grad_sq = lax.psum(grad_local, ('slab', 'phase', 'enc'))  60.7 us
    all_gather x2, blocking collectives, body(): lax.all_gather(low_grad, 'slab', axis=4, tiled=True)  33.1 us
    all_to_all x1, waiting for transfers between devices, body(): lax.all_to_all(coil_maps.reshape(2, coils * readout, zdepth, lines), 'sla...  29.3 us
    ppermute x2, waiting for transfers between devices, with_halo(): after = lax.ppermute(first, axis, down)  12.6 us
    all_to_all x2, starting transfers between devices, body(): lax.all_to_all(partial_rows, 'slab', split_axis=4, concat_axis=3, tiled=T...  9.46 us
    ppermute x2, waiting for transfers between devices, with_halo(): before = lax.ppermute(last, axis, up)  8.38 us
  transfers between devices with their start and end apart: 7, of which 7 were waited for; matrix products, arithmetic and copies ran while one was open for 5% of the time, Pallas kernels for 0%

commit v1 on v0

--- a/solution.py
+++ b/solution.py
@@ -80,13 +80,11 @@
     residual = -(kspace_data.astype(jnp.float32) * sampled)
     image_estimate = jnp.zeros((2, phases, encodings, readout, zdepth, lines), jnp.float32)
     row_count = kspace_data.shape[3]
-    coil_rows = lax.all_to_all(
-        coil_maps.reshape(2, coils * readout, zdepth, lines),
-        "slab",
-        split_axis=1,
-        concat_axis=2,
-        tiled=True,
-    )
+    block = coil_maps.reshape(2, coils * readout, zdepth, lines)
+    n_dev = lax.axis_size("slab")
+    blocks = jnp.stack(jnp.split(block, n_dev, axis=1), axis=0)
+    blocks = lax.all_to_all(blocks, "slab", split_axis=0, concat_axis=0)
+    coil_rows = jnp.concatenate(blocks, axis=2)
     row_columns = (
         lax.axis_index("slab") * row_count + jnp.arange(row_count, dtype=jnp.int32)
     ) % readout

time: 379 us -> 379 us (level)
  no operation moved by 1% of the time
where the time goes in v1:
time: 379 us; the launch traced here: 374 us
  waiting for transfers between devices  155 us (41%)
  blocking collectives  93.8 us (25%)
  other arithmetic  37.3 us (10%)
  matrix products  34.2 us (9%)
  local copies, waits for them, and re-layouts  28.1 us (7%)
  starting transfers between devices  20.1 us (5%)
  between operations  5.09 us (1%)
    all_to_all x2, waiting for transfers between devices, body(): lax.all_to_all(partial_rows, 'slab', split_axis=4, concat_axis=3, tiled=T...  105 us
    psum x2, blocking collectives, body(): grad_sq = lax.psum(grad_local, ('slab', 'phase', 'enc'))  60.7 us
    all_gather x2, blocking collectives, body(): lax.all_gather(low_grad, 'slab', axis=4, tiled=True)  33.2 us
    all_to_all x1, waiting for transfers between devices, body(): blocks = lax.all_to_all(blocks, 'slab', split_axis=0, concat_axis=0)  29.3 us
    ppermute x2, waiting for transfers between devices, with_halo(): after = lax.ppermute(first, axis, down)  12.6 us
    all_to_all x2, starting transfers between devices, body(): lax.all_to_all(partial_rows, 'slab', split_axis=4, concat_axis=3, tiled=T...  9.46 us
    ppermute x2, waiting for transfers between devices, with_halo(): before = lax.ppermute(last, axis, up)  8.38 us
  transfers between devices with their start and end apart: 7, of which 7 were waited for; matrix products, arithmetic and copies ran while one was open for 5% of the time, Pallas kernels for 0%

profile of v1, /device:TPU:0, one launch (start us, length us, event | category | flops | bytes accessed | tf_op | source)
XLA Modules:
  0.0 373.5 jit_solution(14623851110073757523)
XLA Ops:
  3.7 6.5 %all-to-all-start.1 = ((bf16[4,2,24,16,192]{4,3,2,1,0:T(8,128)(2,1)}), bf16[4,2,24,16,192]{4,3,2,1,0:T(8,128)(2,1)}, u32[]{:S(2)}, u32[]{:S(2)}) async-start(bf16[4,2,24,16,192]{4,3,2,1,0:T(8,128)(2,1)} %pad_maximum_fusion.2), calls=%async_computation.1 | async-start | bytes 3145728 | tf_op jit(solution)/shard_map/all_to_all | solution.py:86
  14.4 3.4 copy.53
  17.9 29.3 %all-to-all-done.1 = bf16[4,2,24,16,192]{4,3,2,1,0:T(8,128)(2,1)} async-done(((bf16[4,2,24,16,192]{4,3,2,1,0:T(8,128)(2,1)}), bf16[4,2,24,16,192]{4,3,2,1,0:T(8,128)(2,1)}, u32[]{:S(2)}, u32[]{:S(2)}) %all-to-all-start.1) | async-done | bytes 1179680 | tf_op jit(solution)/shard_map/all_to_all | solution.py:86
  47.2 4.8 %all-to-all-start = ((bf16[2,1,2,24,64,192]{5,3,2,1,0,4:T(8,128)(2,1)}), bf16[2,1,2,24,64,192]{5,3,2,1,0,4:T(8,128)(2,1)}, u32[]{:S(2)}, u32[]{:S(2)}) async-start(bf16[2,1,2,24,64,192]{5,3,2,1,0,4:T(8,128)(2,1)} %copy.53), calls=%async_computation | async-start | bytes 6291456 | tf_op jit(solution)/shard_map/all_to_all | solution.py:95
  56.7 5.5 %collective-permute-done = f32[2,1,2,4,16,192]{5,4,3,2,0,1:T(8,128)S(1)} collective-permute-done((f32[2,1,2,4,16,192]{5,4,3,2,0,1:T(8,128)}, f32[2,1,2,4,16,192]{5,4,3,2,0,1:T(8,128)S(1)}, u32[]{:S(2)}, u32[]{:S(2)}) %collective-permute-start) | collective-permute-done | bytes 196640 | tf_op jit(solution)/shard_map/ppermute | solution.py:20
  62.1 3.9 %collective-permute-done.1 = f32[2,1,2,4,16,192]{5,4,3,2,0,1:T(8,128)} collective-permute-done((f32[2,1,2,4,16,192]{5,4,3,2,0,1:T(8,128)}, f32[2,1,2,4,16,192]{5,4,3,2,0,1:T(8,128)}, u32[]{:S(2)}, u32[]{:S(2)}) %collective-permute-start.1) | collective-permute-done | bytes 196640 | tf_op jit(solution)/shard_map/ppermute | solution.py:19
  73.8 48.5 %all-to-all-done = bf16[2,1,2,24,64,192]{5,3,2,1,0,4:T(8,128)(2,1)} async-done(((bf16[2,1,2,24,64,192]{5,3,2,1,0,4:T(8,128)(2,1)}), bf16[2,1,2,24,64,192]{5,3,2,1,0,4:T(8,128)(2,1)}, u32[]{:S(2)}, u32[]{:S(2)}) %all-to-all-start) | async-done | bytes 2359328 | tf_op jit(solution)/shard_map/all_to_all | solution.py:95
  122.3 3.7 copy.98
  132.7 16.1 %all_gather.6 = bf16[2,1,2,4,64,192]{5,4,3,2,0,1:T(8,128)(2,1)S(1)} all-gather(bf16[2,1,2,4,16,192]{5,4,3,2,0,1:T(8,128)(2,1)S(1)} %get-tuple-element.19), channel_id=1, replica_groups=mesh['pat'=2,'slab'=4,'phase'=2,'enc'=2] {'slab'}, dimensions={4}, use_global_device_ids=true | all-gather | bytes 491520 | tf_op jit(solution)/shard_map/all_gather | solution.py:118
  148.8 2.5 gather_fusion
  151.3 2.5 fusion.2
  166.3 30.6 %all-reduce.3 = (f32[]{:T(128)}, f32[]{:T(128)}) all-reduce(f32[]{:T(128)} %multiply_reduce_fusion.3, f32[]{:T(128)} %multiply_reduce_fusion.1), channel_id=1, replica_groups=mesh['pat'=2,'slab'=4,'phase'=2,'enc'=2] {'slab','phase','enc'}, use_global_device_ids=true, to_apply=%region_3.4 | all-reduce | flops 2 | bytes 16 | tf_op jit(solution)/shard_map/psum | solution.py:115
  198.8 3.6 fusion.3
  205.9 3.4 copy.62
  209.3 4.7 %all-to-all-start.2 = ((bf16[2,1,2,24,64,192]{5,3,2,1,0,4:T(8,128)(2,1)}), bf16[2,1,2,24,64,192]{5,3,2,1,0,4:T(8,128)(2,1)}, u32[]{:S(2)}, u32[]{:S(2)}) async-start(bf16[2,1,2,24,64,192]{5,3,2,1,0,4:T(8,128)(2,1)} %copy.62), calls=%async_computation.2 | async-start | bytes 6291456 | tf_op jit(solution)/shard_map/all_to_all | solution.py:95
  216.1 7.2 %collective-permute-done.2 = f32[2,1,2,4,16,192]{5,4,3,2,0,1:T(8,128)S(1)} collective-permute-done((f32[2,1,2,4,16,192]{5,4,3,2,0,1:T(8,128)S(1)}, f32[2,1,2,4,16,192]{5,4,3,2,0,1:T(8,128)S(1)}, u32[]{:S(2)}, u32[]{:S(2)}) %collective-permute-start.2) | collective-permute-done | bytes 196640 | tf_op jit(solution)/shard_map/ppermute | solution.py:20
  223.2 4.5 %collective-permute-done.3 = f32[2,1,2,4,16,192]{5,4,3,2,0,1:T(8,128)S(1)} collective-permute-done((f32[2,1,2,4,16,192]{5,4,3,2,0,1:T(8,128)S(1)}, f32[2,1,2,4,16,192]{5,4,3,2,0,1:T(8,128)S(1)}, u32[]{:S(2)}, u32[]{:S(2)}) %collective-permute-start.3) | collective-permute-done | bytes 196640 | tf_op jit(solution)/shard_map/ppermute | solution.py:19
  228.8 56.1 %all-to-all-done.2 = bf16[2,1,2,24,64,192]{5,3,2,1,0,4:T(8,128)(2,1)} async-done(((bf16[2,1,2,24,64,192]{5,3,2,1,0,4:T(8,128)(2,1)}), bf16[2,1,2,24,64,192]{5,3,2,1,0,4:T(8,128)(2,1)}, u32[]{:S(2)}, u32[]{:S(2)}) %all-to-all-start.2) | async-done | bytes 2359328 | tf_op jit(solution)/shard_map/all_to_all | solution.py:95
  285.0 3.7 copy.97
  296.6 17.1 %all_gather.7 = bf16[2,1,2,4,64,192]{5,4,3,2,0,1:T(8,128)(2,1)} all-gather(bf16[2,1,2,4,16,192]{5,4,3,2,0,1:T(8,128)(2,1)S(1)} %get-tuple-element.17), channel_id=1, replica_groups=mesh['pat'=2,'slab'=4,'phase'=2,'enc'=2] {'slab'}, dimensions={4}, use_global_device_ids=true | all-gather | bytes 491520 | tf_op jit(solution)/shard_map/all_gather | solution.py:118
  313.7 3.6 gather_fusion.1
  317.2 2.6 fusion.1
  333.2 30.1 %all-reduce.2 = (f32[]{:T(128)}, f32[]{:T(128)}) all-reduce(f32[]{:T(128)} %multiply_reduce_fusion.2, f32[]{:T(128)} %multiply_reduce_fusion), channel_id=1, replica_groups=mesh['pat'=2,'slab'=4,'phase'=2,'enc'=2] {'slab','phase','enc'}, use_global_device_ids=true, to_apply=%region_9.11 | all-reduce | flops 2 | bytes 16 | tf_op jit(solution)/shard_map/psum | solution.py:115
  365.2 7.4 %multiply_subtract_fusion = f32[2,1,2,24,64,192]{5,4,3,2,1,0:T(8,128)} fusion(f32[1,1,2,24,64,192]{5,4,3,2,1,0:T(8,128)} %copy-done.7, f32[1,1,2,24,64,192]{5,4,3,2,1,0:T(8,128)} %copy-done.6, f32[]{:T(128)S(6)} %div.33, f32[2,64,192]{2,1,0:T(8,128)S(1)} %convert_bitcast_fusion.1, f32[1,1,2,24,64,192]{5,4,3,2,1,0:T(8,128)} %copy-done, ...), kind=kLoop, calls=%fused_computation.4 | loop fusion | flops 12976128 | bytes 16613384 | tf_op jit(solution)/shard_map/sub | solution.py:129
  (102 shorter events, 67.3 us)
Async XLA Ops:
  2.1 8.0 %copy-start.16 = (s32[1,2,64,192]{3,2,1,0:T(8,128)S(1)}, s32[1,2,64,192]{3,2,1,0:T(8,128)}, u32[]{:S(2)}) copy-start(s32[1,2,64,192]{3,2,1,0:T(8,128)} %param.7) | copy-start | bytes 294916
  2.1 8.1 %copy-start.5 = (bf16[2,1,2,24,64,192]{5,4,3,2,1,0:T(8,128)(2,1)S(1)}, bf16[2,1,2,24,64,192]{5,4,3,2,1,0:T(8,128)(2,1)}, u32[]{:S(2)}) copy-start(bf16[2,1,2,24,64,192]{5,4,3,2,1,0:T(8,128)(2,1)} %param.5) | copy-start | bytes 7077892
  3.7 43.5 %all-to-all-start.1 = ((bf16[4,2,24,16,192]{4,3,2,1,0:T(8,128)(2,1)}), bf16[4,2,24,16,192]{4,3,2,1,0:T(8,128)(2,1)}, u32[]{:S(2)}, u32[]{:S(2)}) async-start(bf16[4,2,24,16,192]{4,3,2,1,0:T(8,128)(2,1)} %pad_maximum_fusion.2), calls=%async_computation.1 | async-start | bytes 3145728 | tf_op jit(solution)/shard_map/all_to_all | solution.py:86
  47.2 75.1 %all-to-all-start = ((bf16[2,1,2,24,64,192]{5,3,2,1,0,4:T(8,128)(2,1)}), bf16[2,1,2,24,64,192]{5,3,2,1,0,4:T(8,128)(2,1)}, u32[]{:S(2)}, u32[]{:S(2)}) async-start(bf16[2,1,2,24,64,192]{5,3,2,1,0,4:T(8,128)(2,1)} %copy.53), calls=%async_computation | async-start | bytes 6291456 | tf_op jit(solution)/shard_map/all_to_all | solution.py:95
  52.8 9.4 %collective-permute-start = (f32[2,1,2,4,16,192]{5,4,3,2,0,1:T(8,128)}, f32[2,1,2,4,16,192]{5,4,3,2,0,1:T(8,128)S(1)}, u32[]{:S(2)}, u32[]{:S(2)}) collective-permute-start(f32[2,1,2,4,16,192]{5,4,3,2,0,1:T(8,128)} %broadcast_in_dim.8), channel_id=1, source_target_pairs={{2,0},{0,2},{3,1},{1,3},{6,4},{4,6},{7,5},{5,7},{10,8},{8,10},{11,... | collective-permute-start | bytes 589832 | tf_op jit(solution)/shard_map/ppermute | solution.py:20
  54.3 11.8 %collective-permute-start.1 = (f32[2,1,2,4,16,192]{5,4,3,2,0,1:T(8,128)}, f32[2,1,2,4,16,192]{5,4,3,2,0,1:T(8,128)}, u32[]{:S(2)}, u32[]{:S(2)}) collective-permute-start(f32[2,1,2,4,16,192]{5,4,3,2,0,1:T(8,128)} %broadcast_in_dim.8), channel_id=1, source_target_pairs={{0,2},{2,0},{1,3},{3,1},{4,6},{6,4},{5,7},{7,5},{8,10},{10,8},{9,1... | collective-permute-start | bytes 589832 | tf_op jit(solution)/shard_map/ppermute | solution.py:19
  56.6 73.6 %copy-start.1 = (f32[24,4,16,192]{3,2,1,0:T(8,128)}, f32[24,4,16,192]{3,2,1,0:T(8,128)S(1)}, u32[]{:S(2)}) copy-start(f32[24,4,16,192]{3,2,1,0:T(8,128)S(1)} %get-tuple-element.35) | copy-start | bytes 3538948
  56.6 73.6 %copy-start.3 = (f32[24,4,16,192]{3,2,1,0:T(8,128)}, f32[24,4,16,192]{3,2,1,0:T(8,128)S(1)}, u32[]{:S(2)}) copy-start(f32[24,4,16,192]{3,2,1,0:T(8,128)S(1)} %get-tuple-element.36) | copy-start | bytes 3538948
  130.2 2.4 copy-start.15
  151.3 2.5 copy-start.8
  151.3 2.8 copy-start.10
  163.4 2.2 copy-start
  209.3 75.7 %all-to-all-start.2 = ((bf16[2,1,2,24,64,192]{5,3,2,1,0,4:T(8,128)(2,1)}), bf16[2,1,2,24,64,192]{5,3,2,1,0,4:T(8,128)(2,1)}, u32[]{:S(2)}, u32[]{:S(2)}) async-start(bf16[2,1,2,24,64,192]{5,3,2,1,0,4:T(8,128)(2,1)} %copy.62), calls=%async_computation.2 | async-start | bytes 6291456 | tf_op jit(solution)/shard_map/all_to_all | solution.py:95
  214.0 9.2 %collective-permute-start.2 = (f32[2,1,2,4,16,192]{5,4,3,2,0,1:T(8,128)S(1)}, f32[2,1,2,4,16,192]{5,4,3,2,0,1:T(8,128)S(1)}, u32[]{:S(2)}, u32[]{:S(2)}) collective-permute-start(f32[2,1,2,4,16,192]{5,4,3,2,0,1:T(8,128)S(1)} %multiply_subtract_fusion.2), channel_id=1, source_target_pairs={{2,0},{0,2},{3,1},{1,3},{6,4},{4,6},{7,5},{5,7},{10,8},{8,10},{11,... | collective-permute-start | bytes 589832 | tf_op jit(solution)/shard_map/ppermute | solution.py:20
  214.1 13.7 %collective-permute-start.3 = (f32[2,1,2,4,16,192]{5,4,3,2,0,1:T(8,128)S(1)}, f32[2,1,2,4,16,192]{5,4,3,2,0,1:T(8,128)S(1)}, u32[]{:S(2)}, u32[]{:S(2)}) collective-permute-start(f32[2,1,2,4,16,192]{5,4,3,2,0,1:T(8,128)S(1)} %multiply_subtract_fusion.2), channel_id=1, source_target_pairs={{0,2},{2,0},{1,3},{3,1},{4,6},{6,4},{5,7},{7,5},{8,10},{10,8},{9,1... | collective-permute-start | bytes 589832 | tf_op jit(solution)/shard_map/ppermute | solution.py:19
  291.5 1.4 copy-start.2
  291.6 1.9 copy-start.4
  293.4 2.4 copy-start.14
  317.2 2.6 copy-start.9
  317.2 2.8 copy-start.11
  328.6 1.7 copy-start.6
  330.3 2.2 copy-start.7
  330.3 2.2 copy-start.12
  365.2 7.4 %copy-start.13 = (f32[2,1,2,4,16,192]{5,4,3,2,0,1:T(8,128)S(1)}, f32[2,1,2,4,16,192]{5,4,3,2,0,1:T(8,128)}, u32[]{:S(2)}) copy-start(f32[2,1,2,4,16,192]{5,4,3,2,0,1:T(8,128)} %get-tuple-element.18) | copy-start | bytes 589828
